TPU v7x, 512 devices: a whole 4x4x16 slice. The times are simulated.
512 devices in a mesh: dom: 512 (over z, y, x, core).
Axes of the slice: x: 4, y: 4, z: 16, core: 2. Of those that a mesh axis runs over, the one named last changes fastest.
Arguments:
- particles: float32 [512, 2, 256, 128], P('dom'), may hold values from -60 to 60
- offspring: int32 [512], P('dom'), may hold values from 0 to 7, as said below
- noise: float32 [2, 512, 2, 256, 128], P(None, 'dom'), may hold values from -6 to 6
- accept: int32 [2, 512], P(None, 'dom'), may hold values 0 or 1
- observed: float32 [256, 256], replicated, may hold values from -6 to 6
Outputs:
- moved: float32 [512, 2, 256, 128], P('dom')
- misfit: float32 [2, 512], P(None, 'dom')
Inputs may be any that keep to these rules, and one draw needn't show every extreme that they name: `offspring`: the counts sum to 512. Slot s, numbered by the counts' running sum, is filled by a particle at most 3 places from s, and in every draw some slot is filled from exactly 3 places away.
All inputs are finite; a program needn't handle non-finite values. No bound on the sum of `accept` on one device may be relied on, other than what follows from the above.
Results may differ from a plain program's by a relative error of at most 0.0001.
Values sent between devices are 32-bit elements; how exact they have to be, the bound alone decides.
No kernel may reach another device: no remote copies, remote signals or barrier semaphores. Data moves between devices by JAX's collectives and lax.ppermute only.
A program may use at most 64 MiB of HBM per device.

v0:
```python
import math
import jax
import jax.numpy as jnp
from jax import lax
from jax.sharding import PartitionSpec as P

MOVES = 2
SPAN = 3
LOW = 16
time_step = 0.05
viscosity = 0.001
noise_level = 0.5
spectral_scale = 64.0
prior_amplitude = 1.5
step_size = 0.4
highest = lax.Precision.HIGHEST


def carried_in(part, axis, combine, identity):
    place = lax.axis_index(axis)
    gathered = lax.all_gather(part, axis)
    state = jnp.zeros_like(part) + jnp.asarray(identity, part.dtype)

    def one(lap, state):
        return combine(state, lax.dynamic_index_in_dim(gathered, lap, 0, False))

    return lax.fori_loop(0, place, one, state)


def from_behind(value, axis, steps):
    count = lax.axis_size(axis)
    leading, last = (max(0, -steps), min(count, count - steps))
    return lax.ppermute(value, axis, [(source, source + steps) for source in range(leading, last)])


def tables(grid):
    half = grid // 2
    index_a = jnp.arange(grid)
    phase_y = (index_a[:, None] * index_a[None, :] % grid).astype(jnp.float32) * (
        2.0 * math.pi / grid
    )
    cos_y = jnp.cos(phase_y)
    sin_y = jnp.sin(phase_y)
    index_q = jnp.arange(half)
    phase_x = (index_q[:, None] * index_a[None, :] % grid).astype(jnp.float32) * (
        2.0 * math.pi / grid
    )
    weight = jnp.where(index_q == 0, 1.0, 2.0).astype(jnp.float32)[:, None]
    backward_table = (
        jnp.concatenate([weight * jnp.cos(phase_x), -weight * jnp.sin(phase_x)], axis=0)
        / spectral_scale
    )
    fore_table = jnp.concatenate([jnp.cos(phase_x).T, -jnp.sin(phase_x).T], axis=1) * (
        spectral_scale / (grid * grid)
    )
    return (cos_y, sin_y, backward_table, fore_table)


def synthesize(real_part, imag_part, lookup_tables):
    cos_y, sin_y, backward_table, fore_table = lookup_tables
    half = real_part.shape[-1]
    stacked = jnp.concatenate([real_part, imag_part], axis=-1)
    with_cos = jnp.einsum("ap,bpq->baq", cos_y, stacked, precision=highest)
    with_sin = jnp.einsum("ap,bpq->baq", sin_y, stacked, precision=highest)
    rows_re = with_cos[..., :half] - with_sin[..., half:]
    rows_im = with_sin[..., :half] + with_cos[..., half:]
    joined = jnp.concatenate([rows_re, rows_im], axis=-1)
    return jnp.einsum("baq,qc->bac", joined, backward_table, precision=highest)


def analyse(field, lookup_tables):
    cos_y, sin_y, backward_table, fore_table = lookup_tables
    half = field.shape[-1] // 2
    rows = jnp.einsum("bac,cq->baq", field, fore_table, precision=highest)
    with_cos = jnp.einsum("ap,baq->bpq", cos_y, rows, precision=highest)
    with_sin = jnp.einsum("ap,baq->bpq", sin_y, rows, precision=highest)
    return (
        with_cos[..., :half] + with_sin[..., half:],
        with_cos[..., half:] - with_sin[..., :half],
    )


def wavenumbers(grid):
    index_y = jnp.arange(grid)
    wave_y = jnp.where(index_y < grid // 2, index_y, index_y - grid).astype(jnp.float32)[:, None]
    wave_x = jnp.arange(grid // 2).astype(jnp.float32)[None, :]
    return (wave_y, wave_x)


def predicted_state(present_state, observed, lookup_tables):
    grid = present_state.shape[2]
    count = present_state.shape[0]
    wave_y, wave_x = wavenumbers(grid)
    wave_sq = wave_y * wave_y + wave_x * wave_x
    inverse_sq = jnp.where(wave_sq > 0, 1.0 / jnp.maximum(wave_sq, 1.0), 0.0)
    keeper = ((jnp.abs(wave_y) <= grid // 3) & (wave_x <= grid // 3)).astype(jnp.float32)
    damping = 1.0 + time_step * viscosity * wave_sq
    real_part = present_state[:, 0]
    imag_part = present_state[:, 1]
    psi_re = real_part * inverse_sq
    psi_im = imag_part * inverse_sq
    fields = synthesize(
        jnp.concatenate([real_part, -wave_y * psi_im, wave_x * psi_im], axis=0),
        jnp.concatenate([imag_part, wave_y * psi_re, -wave_x * psi_re], axis=0),
        lookup_tables,
    )
    vort = fields[:count]
    products = jnp.concatenate(
        [fields[count : 2 * count] * vort, fields[2 * count :] * vort], axis=0
    )
    flux_re, flux_im = analyse(products, lookup_tables)
    nonlin_re = -(wave_x * flux_im[:count] + wave_y * flux_im[count:]) * keeper
    nonlin_im = (wave_x * flux_re[:count] + wave_y * flux_re[count:]) * keeper
    real_part = (real_part - time_step * nonlin_re) / damping
    imag_part = (imag_part - time_step * nonlin_im) / damping
    final = synthesize(real_part, imag_part, lookup_tables)
    return jnp.sum((final - observed[None]) ** 2, axis=(1, 2)) / (
        2.0 * noise_level * noise_level * grid * grid
    )


def low_modes(block):
    grid = block.shape[-2]
    return jnp.concatenate(
        [block[..., : LOW // 2, :LOW], block[..., grid - LOW // 2 :, :LOW]], axis=-2
    )


def add_counts(earlier, later):
    return earlier + later


def body(particles, offspring, noise, accept, observed):
    per_device = particles.shape[0]
    grid = particles.shape[2]
    devices = lax.axis_size("dom")
    position = lax.axis_index("dom")
    before = carried_in(jnp.sum(offspring), "dom", add_counts, jnp.int32(0))
    finish = before + jnp.cumsum(offspring)
    starts = finish - offspring
    package = (particles, starts.astype(jnp.float32), finish.astype(jnp.float32))
    gathered_values = [package]
    for distance in range(1, SPAN + 1):
        for direction in (1, -1):
            gathered_values.append(
                from_behind((package[0], package[1], package[2]), "dom", direction * distance)
            )
    candidates = jnp.concatenate([item[0] for item in gathered_values], axis=0)
    cand_start = jnp.concatenate([item[1] for item in gathered_values], axis=0)
    cand_end = jnp.concatenate([item[2] for item in gathered_values], axis=0)
    slot_ids = (position * per_device + jnp.arange(per_device, dtype=jnp.int32)).astype(jnp.float32)
    chosen = (
        (cand_start[None, :] <= slot_ids[:, None]) & (slot_ids[:, None] < cand_end[None, :])
    ).astype(jnp.float32)
    present_state = jnp.einsum("sc,cxyz->sxyz", chosen, candidates, precision=highest)
    totals = lax.psum(jnp.sum(low_modes(present_state) ** 2, axis=0), "dom")
    adapted = jnp.sqrt(totals / (per_device * devices) + 1e-06)
    wave_y, wave_x = wavenumbers(grid)
    prior = prior_amplitude / (1.0 + jnp.sqrt(wave_y * wave_y + wave_x * wave_x) / 8.0)
    spread = jnp.stack([prior, prior])
    spread = spread.at[:, : LOW // 2, :LOW].set(adapted[:, : LOW // 2])
    spread = spread.at[:, grid - LOW // 2 :, :LOW].set(adapted[:, LOW // 2 :])
    lookup_tables = tables(grid)
    keep = math.sqrt(1.0 - step_size * step_size)
    score_values = []
    for move in range(MOVES):
        candidate_state = keep * present_state + step_size * spread[None] * noise[move]
        score_values.append(predicted_state(candidate_state, observed, lookup_tables))
        present_state = jnp.where(
            accept[move][:, None, None, None] == 1, candidate_state, present_state
        )
    return (present_state, jnp.stack(score_values))


def solution(mesh):
    return jax.shard_map(
        body,
        mesh=mesh,
        in_specs=(
            P("dom", None, None, None),
            P("dom"),
            P(None, "dom", None, None, None),
            P(None, "dom"),
            P(),
        ),
        out_specs=(P("dom", None, None, None), P(None, "dom")),
        check_vma=False,
    )
```

profile of v0, /device:TPU:1, one launch (start us, length us, event | category | flops | bytes accessed | tf_op | source)
XLA Modules:
  0.0 980.4 jit_solution(8580837013161240498)
XLA Ops:
  1.4 111.0 %all-reduce = s32[512]{0:T(512)S(1)} all-reduce(s32[512]{0:T(512)S(1)} %dynamic-update-slice.8), channel_id=1, replica_groups=mesh['dom'=512] {'dom'}, use_global_device_ids=true, to_apply=%add | all-reduce | flops 512 | bytes 4096
  113.7 8.1 collective-permute-start.10
  123.1 3.1 collective-permute-start.12
  126.2 1.9 collective-permute-start.13
  128.2 7.6 collective-permute-start.14
  141.4 3.9 collective-permute-start.6
  145.3 2.7 collective-permute-start.7
  148.1 6.3 collective-permute-start.8
  155.6 7.6 collective-permute-start
  163.2 2.8 collective-permute-start.1
  166.0 3.8 concatenate.77
  169.9 7.6 collective-permute-start.2
  178.7 11.9 %collective-permute-start.4 = (f32[1]{0:T(128)}, f32[1]{0:T(128)}, u32[]{:S(2)}, u32[]{:S(2)}) collective-permute-start(f32[1]{0:T(128)} %convert_element_type.174), channel_id=1, source_target_pairs={{0,3},{1,4},{2,5},{3,6},{4,7},{5,8},{6,9},{7,10},{8,11},{9,12},{10... | collective-permute-start | bytes 20 | tf_op jit(solution)/shard_map/ppermute | solution.py:33
  193.2 4.5 collective-permute-done.5
  197.7 9.1 collective-permute-start.16
  206.8 3.7 concatenate.76
  215.7 5.3 collective-permute-done.17
  221.0 2.1 fusion
  223.4 725.5 %psum.7 = f32[2,16,16]{1,2,0:T(8,128)S(1)} all-reduce(f32[2,16,16]{1,2,0:T(8,128)S(1)} %maximum_multiply_fusion.6), channel_id=1, replica_groups=mesh['dom'=512] {'dom'}, use_global_device_ids=true, to_apply=%region_2.3 | all-reduce | flops 512 | bytes 4096 | tf_op jit(solution)/shard_map/psum | solution.py:156
  951.2 1.8 convolution_bitcast_fusion.1
  953.0 1.8 convolution_bitcast_fusion
  954.9 1.4 fusion.8
  957.1 1.6 convolution_bitcast_fusion.4
  958.6 1.6 convolution_bitcast_fusion.5
  960.2 1.8 convolution_bitcast_fusion.3
  962.0 2.0 convolution_bitcast_fusion.2
  964.1 1.4 fusion.4
  966.2 1.6 convolution_bitcast_fusion.6
  967.8 1.6 convolution_bitcast_fusion.7
  969.7 1.4 convolution_bitcast_fusion.11
  971.1 1.4 convolution_bitcast_fusion.10
  973.8 1.4 convolution_bitcast_fusion.8
  (81 shorter events, 27.7 us)
Async XLA Ops:
  0.6 138.0 %copy-start.1 = (s32[2,1]{0,1:T(1,128)S(1)}, s32[2,1]{0,1:T(1,128)}, u32[]{:S(2)}) copy-start(s32[2,1]{0,1:T(1,128)} %param.14) | copy-start | bytes 28
  113.7 27.7 %collective-permute-start.10 = (f32[1]{0:T(128)}, f32[1]{0:T(128)}, u32[]{:S(2)}, u32[]{:S(2)}) collective-permute-start(f32[1]{0:T(128)} %convert_element_type.176), channel_id=1, source_target_pairs={{0,3},{1,4},{2,5},{3,6},{4,7},{5,8},{6,9},{7,10},{8,11},{9,12},{10... | collective-permute-start | bytes 20 | tf_op jit(solution)/shard_map/ppermute | solution.py:33
  121.8 23.5 %collective-permute-start.11 = (f32[1]{0:T(128)}, f32[1]{0:T(128)}, u32[]{:S(2)}, u32[]{:S(2)}) collective-permute-start(f32[1]{0:T(128)} %convert_element_type.176), channel_id=1, source_target_pairs={{3,0},{4,1},{5,2},{6,3},{7,4},{8,5},{9,6},{10,7},{11,8},{12,9},{13... | collective-permute-start | bytes 20 | tf_op jit(solution)/shard_map/ppermute | solution.py:33
  123.1 87.4 %collective-permute-start.12 = (f32[1,2,256,128]{3,2,1,0:T(8,128)}, f32[1,2,256,128]{3,2,1,0:T(8,128)}, u32[]{:S(2)}, u32[]{:S(2)}) collective-permute-start(f32[1,2,256,128]{3,2,1,0:T(8,128)} %param.11), channel_id=1, source_target_pairs={{0,1},{1,2},{2,3},{3,4},{4,5},{5,6},{6,7},{7,8},{8,9},{9,10},{10,1... | collective-permute-start | bytes 786440 | tf_op jit(solution)/shard_map/ppermute | solution.py:33
  126.2 86.5 %collective-permute-start.13 = (f32[1,2,256,128]{3,2,1,0:T(8,128)}, f32[1,2,256,128]{3,2,1,0:T(8,128)}, u32[]{:S(2)}, u32[]{:S(2)}) collective-permute-start(f32[1,2,256,128]{3,2,1,0:T(8,128)} %param.11), channel_id=1, source_target_pairs={{1,0},{2,1},{3,2},{4,3},{5,4},{6,5},{7,6},{8,7},{9,8},{10,9},{11,1... | collective-permute-start | bytes 786440 | tf_op jit(solution)/shard_map/ppermute | solution.py:33
  128.2 85.5 %collective-permute-start.14 = (f32[1,2,256,128]{3,2,1,0:T(8,128)}, f32[1,2,256,128]{3,2,1,0:T(8,128)}, u32[]{:S(2)}, u32[]{:S(2)}) collective-permute-start(f32[1,2,256,128]{3,2,1,0:T(8,128)} %param.11), channel_id=1, source_target_pairs={{0,2},{1,3},{2,4},{3,5},{4,6},{5,7},{6,8},{7,9},{8,10},{9,11},{10,... | collective-permute-start | bytes 786440 | tf_op jit(solution)/shard_map/ppermute | solution.py:33
  141.4 6.7 collective-permute-start.6
  145.3 9.0 collective-permute-start.7
  148.1 7.6 collective-permute-start.8
  154.3 8.9 collective-permute-start.9
  155.6 14.2 %collective-permute-start = (f32[1]{0:T(128)}, f32[1]{0:T(128)}, u32[]{:S(2)}, u32[]{:S(2)}) collective-permute-start(f32[1]{0:T(128)} %convert_element_type.174), channel_id=1, source_target_pairs={{0,1},{1,2},{2,3},{3,4},{4,5},{5,6},{6,7},{7,8},{8,9},{9,10},{10,1... | collective-permute-start | bytes 20 | tf_op jit(solution)/shard_map/ppermute | solution.py:33
  163.2 14.3 %collective-permute-start.1 = (f32[1]{0:T(128)}, f32[1]{0:T(128)}, u32[]{:S(2)}, u32[]{:S(2)}) collective-permute-start(f32[1]{0:T(128)} %convert_element_type.174), channel_id=1, source_target_pairs={{1,0},{2,1},{3,2},{4,3},{5,4},{6,5},{7,6},{8,7},{9,8},{10,9},{11,1... | collective-permute-start | bytes 20 | tf_op jit(solution)/shard_map/ppermute | solution.py:33
  169.9 8.9 collective-permute-start.2
  177.4 13.2 %collective-permute-start.3 = (f32[1]{0:T(128)}, f32[1]{0:T(128)}, u32[]{:S(2)}, u32[]{:S(2)}) collective-permute-start(f32[1]{0:T(128)} %convert_element_type.174), channel_id=1, source_target_pairs={{2,0},{3,1},{4,2},{5,3},{6,4},{7,5},{8,6},{9,7},{10,8},{11,9},{12,... | collective-permute-start | bytes 20 | tf_op jit(solution)/shard_map/ppermute | solution.py:33
  178.7 13.2 %collective-permute-start.4 = (f32[1]{0:T(128)}, f32[1]{0:T(128)}, u32[]{:S(2)}, u32[]{:S(2)}) collective-permute-start(f32[1]{0:T(128)} %convert_element_type.174), channel_id=1, source_target_pairs={{0,3},{1,4},{2,5},{3,6},{4,7},{5,8},{6,9},{7,10},{8,11},{9,12},{10... | collective-permute-start | bytes 20 | tf_op jit(solution)/shard_map/ppermute | solution.py:33
  190.6 7.1 collective-permute-start.5
  191.9 22.8 %collective-permute-start.15 = (f32[1,2,256,128]{3,2,1,0:T(8,128)}, f32[1,2,256,128]{3,2,1,0:T(8,128)S(1)}, u32[]{:S(2)}, u32[]{:S(2)}) collective-permute-start(f32[1,2,256,128]{3,2,1,0:T(8,128)} %param.11), channel_id=1, source_target_pairs={{2,0},{3,1},{4,2},{5,3},{6,4},{7,5},{8,6},{9,7},{10,8},{11,9},{12,... | collective-permute-start | bytes 786440 | tf_op jit(solution)/shard_map/ppermute | solution.py:33
  197.7 17.0 %collective-permute-start.16 = (f32[1,2,256,128]{3,2,1,0:T(8,128)}, f32[1,2,256,128]{3,2,1,0:T(8,128)}, u32[]{:S(2)}, u32[]{:S(2)}) collective-permute-start(f32[1,2,256,128]{3,2,1,0:T(8,128)} %param.11), channel_id=1, source_target_pairs={{0,3},{1,4},{2,5},{3,6},{4,7},{5,8},{6,9},{7,10},{8,11},{9,12},{10... | collective-permute-start | bytes 786440 | tf_op jit(solution)/shard_map/ppermute | solution.py:33
  210.5 10.6 %collective-permute-start.17 = (f32[1,2,256,128]{3,2,1,0:T(8,128)}, f32[1,2,256,128]{3,2,1,0:T(8,128)S(1)}, u32[]{:S(2)}, u32[]{:S(2)}) collective-permute-start(f32[1,2,256,128]{3,2,1,0:T(8,128)} %param.11), channel_id=1, source_target_pairs={{3,0},{4,1},{5,2},{6,3},{7,4},{8,5},{9,6},{10,7},{11,8},{12,9},{13... | collective-permute-start | bytes 786440 | tf_op jit(solution)/shard_map/ppermute | solution.py:33
  972.5 2.8 copy-start
where the time goes:
time: 999 us; the launch traced here: 980 us
  blocking collectives  836 us (84%)
  starting transfers between devices  80.4 us (8%)
  matrix products  27.6 us (3%)
  local copies, waits for them, and re-layouts  18.2 us (2%)
    psum x1, blocking collectives, body(): totals = lax.psum(jnp.sum(low_modes(present_state) ** 2, axis=0), 'dom')  725 us
    unnamed x1, blocking collectives  111 us
    ppermute x18, starting transfers between devices, from_behind(): lax.ppermute(value, axis, [(source, source + steps) for source in range(l...  80.4 us
  transfers between devices with their start and end apart: 18, of which 2 were waited for; matrix products, arithmetic and copies ran while one was open for 2% of the time, Pallas kernels for 0%

commit v1 on v0

--- a/solution.py
+++ b/solution.py
@@ -14,6 +14,11 @@
 prior_amplitude = 1.5
 step_size = 0.4
 highest = lax.Precision.HIGHEST
+
+
+def summed_here(value, mesh_axis):
+    parts = lax.all_gather(value, mesh_axis)
+    return jnp.sum(parts, axis=0)
 
 
 def carried_in(part, axis, combine, identity):
@@ -153,7 +158,7 @@
         (cand_start[None, :] <= slot_ids[:, None]) & (slot_ids[:, None] < cand_end[None, :])
     ).astype(jnp.float32)
     present_state = jnp.einsum("sc,cxyz->sxyz", chosen, candidates, precision=highest)
-    totals = lax.psum(jnp.sum(low_modes(present_state) ** 2, axis=0), "dom")
+    totals = summed_here(jnp.sum(low_modes(present_state) ** 2, axis=0), "dom")
     adapted = jnp.sqrt(totals / (per_device * devices) + 1e-06)
     wave_y, wave_x = wavenumbers(grid)
     prior = prior_amplitude / (1.0 + jnp.sqrt(wave_y * wave_y + wave_x * wave_x) / 8.0)

time: 999 us -> 1170 us (1.17); the launches traced: 980 us -> 1170 us
  waiting for transfers between devices: 9.8 us -> 908 us
  blocking collectives: 836 us -> 106 us
  between operations: 4.48 us -> 17.9 us
    all_gather x0 -> x1, waiting for transfers between devices: none -> 893 us  [summed_here(): parts = lax.all_gather(value, mesh_axis)]
    psum x1 -> x0, blocking collectives: 725 us -> none  [body(): totals = lax.psum(jnp.sum(low_modes(present_state) ** 2, axis=0), 'dom')]
  transfers between devices with their start and end apart: 18 -> 19, of which waited for: 2 -> 4; matrix products, arithmetic and copies ran while one was open for 2% -> 1% of each run, Pallas kernels for 0% -> 0%
where the time goes in v1:
time: 1170 us
  waiting for transfers between devices  908 us (78%)
  blocking collectives  106 us (9%)
  starting transfers between devices  86.3 us (7%)
  matrix products  27.5 us (2%)
  between operations  17.9 us (2%)
  local copies, waits for them, and re-layouts  14.3 us (1%)
    all_gather x1, waiting for transfers between devices, summed_here(): parts = lax.all_gather(value, mesh_axis)  893 us
    unnamed x1, blocking collectives  106 us
    ppermute x18, starting transfers between devices, from_behind(): lax.ppermute(value, axis, [(source, source + steps) for source in range(l...  86.3 us
  transfers between devices with their start and end apart: 19, of which 4 were waited for; matrix products, arithmetic and copies ran while one was open for 1% of the time, Pallas kernels for 0%

profile of v1, /device:TPU:1, one launch (start us, length us, event | category | flops | bytes accessed | tf_op | source)
XLA Modules:
  0.0 1167.5 jit_solution(10788840636994203056)
XLA Ops:
  7.2 4.5 collective-permute-start.12
  11.7 5.6 collective-permute-start.13
  18.1 106.4 %all-reduce = s32[512]{0:T(512)S(1)} all-reduce(s32[512]{0:T(512)S(1)} %dynamic-update-slice.8), channel_id=1, replica_groups=mesh['dom'=512] {'dom'}, use_global_device_ids=true, to_apply=%add | all-reduce | flops 512 | bytes 4096
  124.5 1.4 while.12
  125.8 8.5 collective-permute-start.10
  135.7 7.5 collective-permute-start.14
  144.2 5.4 collective-permute-start.6
  149.6 2.7 collective-permute-start.7
  152.3 6.5 collective-permute-start.8
  160.1 7.6 collective-permute-start
  167.7 2.7 collective-permute-start.1
  170.4 3.8 concatenate.79
  174.2 5.9 collective-permute-start.2
  181.4 13.6 %collective-permute-start.4 = (f32[1]{0:T(128)}, f32[1]{0:T(128)}, u32[]{:S(2)}, u32[]{:S(2)}) collective-permute-start(f32[1]{0:T(128)} %convert_element_type.174), channel_id=1, source_target_pairs={{0,3},{1,4},{2,5},{3,6},{4,7},{5,8},{6,9},{7,10},{8,11},{9,12},{10... | collective-permute-start | bytes 20 | tf_op jit(solution)/shard_map/ppermute | solution.py:38
  197.6 4.5 collective-permute-done.5
  202.1 8.1 collective-permute-start.16
  210.2 3.8 concatenate.78
  215.6 10.1 collective-permute-done.17
  225.8 2.1 fusion
  232.5 892.6 %all-gather.2.cloned.1.call-done = f32[512,2,16,16]{3,2,1,0:T(8,128)} async-done(((f32[1,2,16,16]{3,2,1,0:T(8,128)}), f32[512,2,16,16]{3,2,1,0:T(8,128)}) %all-gather.2.cloned.1.call-update) | async-done | bytes 1048592 | tf_op jit(solution)/shard_map/all_gather | solution.py:20
  1125.1 4.0 reduce_sum.27
  1131.6 1.8 convolution_bitcast_fusion.1
  1133.3 1.8 convolution_bitcast_fusion
  1135.2 1.4 fusion.8
  1137.4 1.6 convolution_bitcast_fusion.4
  1138.9 1.6 convolution_bitcast_fusion.5
  1140.5 1.8 convolution_bitcast_fusion.3
  1142.2 2.0 convolution_bitcast_fusion.2
  1144.4 1.4 fusion.4
  1146.5 1.6 convolution_bitcast_fusion.6
  1148.1 1.6 convolution_bitcast_fusion.7
  1151.4 1.4 convolution_bitcast_fusion.10
  (88 shorter events, 25.5 us)
Async XLA Ops:
  7.2 1117.9 %all-gather.2.cloned.1.call-start = ((), (), s32[]{:S(2)}) async-start(), calls=%async_computation | async-start | bytes 8404992 | tf_op jit(solution)/shard_map/all_gather | solution.py:20
  7.2 206.7 %collective-permute-start.12 = (f32[1,2,256,128]{3,2,1,0:T(8,128)}, f32[1,2,256,128]{3,2,1,0:T(8,128)S(1)}, u32[]{:S(2)}, u32[]{:S(2)}) collective-permute-start(f32[1,2,256,128]{3,2,1,0:T(8,128)} %param.11), channel_id=1, source_target_pairs={{0,1},{1,2},{2,3},{3,4},{4,5},{5,6},{6,7},{7,8},{8,9},{9,10},{10,1... | collective-permute-start | bytes 786440 | tf_op jit(solution)/shard_map/ppermute | solution.py:38
  11.7 203.6 %collective-permute-start.13 = (f32[1,2,256,128]{3,2,1,0:T(8,128)}, f32[1,2,256,128]{3,2,1,0:T(8,128)S(1)}, u32[]{:S(2)}, u32[]{:S(2)}) collective-permute-start(f32[1,2,256,128]{3,2,1,0:T(8,128)} %param.11), channel_id=1, source_target_pairs={{1,0},{2,1},{3,2},{4,3},{5,4},{6,5},{7,6},{8,7},{9,8},{10,9},{11,1... | collective-permute-start | bytes 786440 | tf_op jit(solution)/shard_map/ppermute | solution.py:38
  125.8 18.3 %collective-permute-start.10 = (f32[1]{0:T(128)}, f32[1]{0:T(128)}, u32[]{:S(2)}, u32[]{:S(2)}) collective-permute-start(f32[1]{0:T(128)} %convert_element_type.176), channel_id=1, source_target_pairs={{0,3},{1,4},{2,5},{3,6},{4,7},{5,8},{6,9},{7,10},{8,11},{9,12},{10... | collective-permute-start | bytes 20 | tf_op jit(solution)/shard_map/ppermute | solution.py:38
  134.4 15.2 %collective-permute-start.11 = (f32[1]{0:T(128)}, f32[1]{0:T(128)}, u32[]{:S(2)}, u32[]{:S(2)}) collective-permute-start(f32[1]{0:T(128)} %convert_element_type.176), channel_id=1, source_target_pairs={{3,0},{4,1},{5,2},{6,3},{7,4},{8,5},{9,6},{10,7},{11,8},{12,9},{13... | collective-permute-start | bytes 20 | tf_op jit(solution)/shard_map/ppermute | solution.py:38
  135.7 79.7 %collective-permute-start.14 = (f32[1,2,256,128]{3,2,1,0:T(8,128)}, f32[1,2,256,128]{3,2,1,0:T(8,128)S(1)}, u32[]{:S(2)}, u32[]{:S(2)}) collective-permute-start(f32[1,2,256,128]{3,2,1,0:T(8,128)} %param.11), channel_id=1, source_target_pairs={{0,2},{1,3},{2,4},{3,5},{4,6},{5,7},{6,8},{7,9},{8,10},{9,11},{10,... | collective-permute-start | bytes 786440 | tf_op jit(solution)/shard_map/ppermute | solution.py:38
  144.2 8.1 collective-permute-start.6
  149.6 9.2 collective-permute-start.7
  152.3 7.8 collective-permute-start.8
  158.8 8.9 collective-permute-start.9
  160.1 14.1 %collective-permute-start = (f32[1]{0:T(128)}, f32[1]{0:T(128)}, u32[]{:S(2)}, u32[]{:S(2)}) collective-permute-start(f32[1]{0:T(128)} %convert_element_type.174), channel_id=1, source_target_pairs={{0,1},{1,2},{2,3},{3,4},{4,5},{5,6},{6,7},{7,8},{8,9},{9,10},{10,1... | collective-permute-start | bytes 20 | tf_op jit(solution)/shard_map/ppermute | solution.py:38
  167.7 12.4 %collective-permute-start.1 = (f32[1]{0:T(128)}, f32[1]{0:T(128)}, u32[]{:S(2)}, u32[]{:S(2)}) collective-permute-start(f32[1]{0:T(128)} %convert_element_type.174), channel_id=1, source_target_pairs={{1,0},{2,1},{3,2},{4,3},{5,4},{6,5},{7,6},{8,7},{9,8},{10,9},{11,1... | collective-permute-start | bytes 20 | tf_op jit(solution)/shard_map/ppermute | solution.py:38
  174.2 7.2 collective-permute-start.2
  180.1 14.9 %collective-permute-start.3 = (f32[1]{0:T(128)}, f32[1]{0:T(128)}, u32[]{:S(2)}, u32[]{:S(2)}) collective-permute-start(f32[1]{0:T(128)} %convert_element_type.174), channel_id=1, source_target_pairs={{2,0},{3,1},{4,2},{5,3},{6,4},{7,5},{8,6},{9,7},{10,8},{11,9},{12,... | collective-permute-start | bytes 20 | tf_op jit(solution)/shard_map/ppermute | solution.py:38
  181.4 14.9 %collective-permute-start.4 = (f32[1]{0:T(128)}, f32[1]{0:T(128)}, u32[]{:S(2)}, u32[]{:S(2)}) collective-permute-start(f32[1]{0:T(128)} %convert_element_type.174), channel_id=1, source_target_pairs={{0,3},{1,4},{2,5},{3,6},{4,7},{5,8},{6,9},{7,10},{8,11},{9,12},{10... | collective-permute-start | bytes 20 | tf_op jit(solution)/shard_map/ppermute | solution.py:38
  195.0 7.1 collective-permute-start.5
  196.3 19.1 %collective-permute-start.15 = (f32[1,2,256,128]{3,2,1,0:T(8,128)}, f32[1,2,256,128]{3,2,1,0:T(8,128)S(1)}, u32[]{:S(2)}, u32[]{:S(2)}) collective-permute-start(f32[1,2,256,128]{3,2,1,0:T(8,128)} %param.11), channel_id=1, source_target_pairs={{2,0},{3,1},{4,2},{5,3},{6,4},{7,5},{8,6},{9,7},{10,8},{11,9},{12,... | collective-permute-start | bytes 786440 | tf_op jit(solution)/shard_map/ppermute | solution.py:38
  202.1 13.5 %collective-permute-start.16 = (f32[1,2,256,128]{3,2,1,0:T(8,128)}, f32[1,2,256,128]{3,2,1,0:T(8,128)S(1)}, u32[]{:S(2)}, u32[]{:S(2)}) collective-permute-start(f32[1,2,256,128]{3,2,1,0:T(8,128)} %param.11), channel_id=1, source_target_pairs={{0,3},{1,4},{2,5},{3,6},{4,7},{5,8},{6,9},{7,10},{8,11},{9,12},{10... | collective-permute-start | bytes 786440 | tf_op jit(solution)/shard_map/ppermute | solution.py:38
  213.9 11.8 %collective-permute-start.17 = (f32[1,2,256,128]{3,2,1,0:T(8,128)}, f32[1,2,256,128]{3,2,1,0:T(8,128)S(1)}, u32[]{:S(2)}, u32[]{:S(2)}) collective-permute-start(f32[1,2,256,128]{3,2,1,0:T(8,128)} %param.11), channel_id=1, source_target_pairs={{3,0},{4,1},{5,2},{6,3},{7,4},{8,5},{9,6},{10,7},{11,8},{12,9},{13... | collective-permute-start | bytes 786440 | tf_op jit(solution)/shard_map/ppermute | solution.py:38
  215.6 13.2 %copy-start.1 = (f32[2,1,2,256,128]{4,3,2,1,0:T(8,128)S(1)}, f32[2,1,2,256,128]{4,3,2,1,0:T(8,128)}, u32[]{:S(2)}) copy-start(f32[2,1,2,256,128]{4,3,2,1,0:T(8,128)} %param.13) | copy-start | bytes 1572868
  227.9 1.3 copy-start.2
  1152.7 2.8 copy-start
Sparse Core Ops, SparseCore 0:
  229.0 896.0 all-gather.1
